TPU v7x, 8 devices: a whole 2x2x1 slice. The times are simulated.
8 devices in a mesh: stage: 2 (over z, y), expert: 4 (over x, core).
Axes of the slice: x: 2, y: 2, z: 1, core: 2. Of those that a mesh axis runs over, the one named last changes fastest.
Arguments:
- w_gate: bfloat16 [2, 16, 2560, 1536], P('stage', 'expert')
- w_up: bfloat16 [2, 16, 2560, 1536], P('stage', 'expert')
- w_down: bfloat16 [2, 16, 1536, 2560], P('stage', 'expert')
- x: bfloat16 [2048, 2560], P(('stage', 'expert'))
- expert_ids: int32 [2, 2048, 6], P(None, ('stage', 'expert'))
- gates: float32 [2, 2048, 6], P(None, ('stage', 'expert'))
Outputs:
- output 1: bfloat16 [2, 16, 2560, 3072], P(None, ('stage', 'expert'))
- output 2: bfloat16 [2, 16, 1536, 2560], P(None, ('stage', 'expert'))
- output 3: float32 [2, 2048, 2560], P(None, ('stage', 'expert'))
All inputs are finite; a program needn't handle non-finite values.
Results may differ from a plain program's by a relative error of at most 0.001.
Values are sent between devices in bfloat16 or wider.
A program may use at most 1 GiB of HBM per device.

v0:
```python
import jax
import jax.numpy as jnp
from jax import lax
from jax.sharding import PartitionSpec as P

NORM_EPS = 1e-6
FLAT = ("stage", "expert")


def norm_rows(hidden):
    return (hidden * lax.rsqrt(jnp.mean(hidden * hidden, axis=-1, keepdims=True) + NORM_EPS)).astype(jnp.bfloat16)


def slot_table(layer_ids, n_experts, capacity):
    flat_ids = layer_ids.reshape(-1)
    onehot = (flat_ids[:, None] == jnp.arange(n_experts)[None, :]).astype(jnp.int32)
    pair_rank = jnp.sum(onehot * jnp.cumsum(onehot, axis=0), axis=-1) - 1
    return flat_ids * capacity + pair_rank


def moe_layer(hidden, layer_w13, layer_down, layer_ids, layer_mix, capacity, dev_count):
    tok_dev, model_width = hidden.shape
    top_k = layer_ids.shape[-1]
    exp_dev = layer_w13.shape[0]
    expert_width = layer_down.shape[1]
    n_experts = exp_dev * dev_count
    normed = norm_rows(hidden)
    slot_pos = slot_table(layer_ids, n_experts, capacity)
    pair_tok = jnp.arange(tok_dev * top_k, dtype=jnp.int32) // top_k
    source_row = jnp.zeros((n_experts * capacity,), jnp.int32).at[slot_pos].set(pair_tok)
    outbound = jnp.take(normed, source_row, axis=0).reshape(dev_count, exp_dev, capacity, model_width)
    inbound = lax.all_to_all(outbound, FLAT, 0, 0, tiled=True)
    projected = jnp.einsum("nxcd,xdg->nxcg", inbound, layer_w13, preferred_element_type=jnp.float32)
    activated = (jax.nn.silu(projected[..., :expert_width]) * projected[..., expert_width:]).astype(jnp.bfloat16)
    expert_out = jnp.einsum("nxcf,xfd->nxcd", activated, layer_down, preferred_element_type=jnp.float32).astype(jnp.bfloat16)
    returned = lax.all_to_all(expert_out, FLAT, 0, 0, tiled=True)
    picked = jnp.take(returned.reshape(n_experts * capacity, model_width), slot_pos, axis=0)
    picked = picked.reshape(tok_dev, top_k, model_width).astype(jnp.float32)
    return hidden + jnp.sum(layer_mix[..., None] * picked, axis=1)


def hand_over(gate_loc, up_loc, down_loc, n_stage, n_group):
    stage_idx = lax.axis_index("stage")
    flat_idx = stage_idx * n_group + lax.axis_index("expert")
    lay_stage = gate_loc.shape[0]
    exp_dev = gate_loc.shape[1] // n_stage
    fused_loc = jnp.concatenate([gate_loc, up_loc], axis=-1)
    fused_new = jnp.zeros((lay_stage * n_stage, exp_dev) + fused_loc.shape[2:], fused_loc.dtype)
    down_new = jnp.zeros((lay_stage * n_stage, exp_dev) + down_loc.shape[2:], down_loc.dtype)
    for round_idx in range(n_stage):
        pair_list = [(src_stage * n_group + src_group, src_group * n_stage + (src_stage + round_idx) % n_stage) for src_stage in range(n_stage) for src_group in range(n_group)]
        piece_idx = (stage_idx + round_idx) % n_stage
        fused_in = lax.ppermute(lax.dynamic_slice_in_dim(fused_loc, piece_idx * exp_dev, exp_dev, axis=1), FLAT, pair_list)
        down_in = lax.ppermute(lax.dynamic_slice_in_dim(down_loc, piece_idx * exp_dev, exp_dev, axis=1), FLAT, pair_list)
        from_stage = (flat_idx % n_stage - round_idx) % n_stage
        fused_new = lax.dynamic_update_slice_in_dim(fused_new, fused_in, from_stage * lay_stage, axis=0)
        down_new = lax.dynamic_update_slice_in_dim(down_new, down_in, from_stage * lay_stage, axis=0)
    return fused_new, down_new


def solution(mesh):
    n_stage = mesh.shape["stage"]
    n_group = mesh.shape["expert"]
    dev_count = n_stage * n_group

    def per_device(gate_loc, up_loc, down_loc, x_loc, ids_loc, mix_loc):
        fused_new, down_new = hand_over(gate_loc, up_loc, down_loc, n_stage, n_group)
        n_experts = fused_new.shape[1] * dev_count
        capacity = 3 * x_loc.shape[0] * ids_loc.shape[-1] // (2 * n_experts)
        hidden = x_loc.astype(jnp.float32)
        layer_outs = []
        for layer_idx in range(fused_new.shape[0]):
            hidden = moe_layer(hidden, fused_new[layer_idx], down_new[layer_idx], ids_loc[layer_idx], mix_loc[layer_idx], capacity, dev_count)
            layer_outs.append(hidden)
        return fused_new, down_new, jnp.stack(layer_outs)

    weight_spec = P("stage", "expert")
    token_spec = P(None, FLAT)
    return jax.shard_map(per_device, mesh=mesh, in_specs=(weight_spec, weight_spec, weight_spec, P(FLAT), token_spec, token_spec), out_specs=(token_spec, token_spec, token_spec), check_vma=False)
```

profile of v0, /device:TPU:0, one launch (start us, length us, event | category | flops | bytes accessed | tf_op | source)
XLA Modules:
  0.0 1986.2 jit_solution(12968982124369621379)
XLA Ops:
  0.7 21.5 %constant_dynamic-update-slice_fusion.1 = bf16[1,4,2560,3072]{3,2,1,0:T(8,128)(2,1)} fusion(bf16[1,4,2560,1536]{3,2,1,0:T(8,128)(2,1)} %param.10), kind=kLoop, calls=%fused_computation.88 | loop fusion | bytes 62914560
  22.2 21.5 %constant_dynamic-update-slice_fusion = bf16[1,4,2560,3072]{3,2,1,0:T(8,128)(2,1)} fusion(bf16[1,4,2560,3072]{3,2,1,0:T(8,128)(2,1)} %constant_dynamic-update-slice_fusion.1, bf16[1,4,2560,1536]{3,2,1,0:T(8,128)(2,1)} %param.11), kind=kLoop, calls=%fused_computation.87 | loop fusion | bytes 62914560 | tf_op jit(solution)/shard_map/concatenate | solution.py:47
  43.7 41.2 %constant_dynamic-slice_fusion.2 = (bf16[1,2,2560,3072]{3,2,1,0:T(8,128)(2,1)}, bf16[1,2,2560,3072]{3,2,1,0:T(8,128)(2,1)}) fusion(bf16[1,4,2560,3072]{3,2,1,0:T(8,128)(2,1)} %constant_dynamic-update-slice_fusion, s32[]{:T(128)S(6)} %select_n.88, s32[]{:T(128)S(6)} %select_n.83), kind=kLoop, calls=%fused_computation.96 | loop fusion | bytes 125829128 | tf_op jit(solution)/shard_map/dynamic_slice | solution.py:53
  84.9 235.9 %collective-permute-start = (bf16[1,2,2560,3072]{3,2,1,0:T(8,128)(2,1)}, bf16[1,2,2560,3072]{3,2,1,0:T(8,128)(2,1)}, u32[]{:S(2)}, u32[]{:S(2)}) collective-permute-start(bf16[1,2,2560,3072]{3,2,1,0:T(8,128)(2,1)} %get-tuple-element.10), channel_id=1, source_target_pairs={{0,0},{1,2},{2,4},{3,6},{4,1},{5,3},{6,5},{7,7}} | collective-permute-start | bytes 94371848 | tf_op jit(solution)/shard_map/ppermute | solution.py:53
  320.9 21.8 %constant_dynamic-slice_fusion = (bf16[1,2,1536,2560]{3,2,1,0:T(8,128)(2,1)}, bf16[1,2,1536,2560]{3,2,1,0:T(8,128)(2,1)}) fusion(bf16[1,4,1536,2560]{3,2,1,0:T(8,128)(2,1)} %param.12, s32[]{:T(128)S(6)} %select_n.88, s32[]{:T(128)S(6)} %select_n.83), kind=kLoop, calls=%fused_computation.92 | loop fusion | bytes 62914568 | tf_op jit(solution)/shard_map/dynamic_slice | solution.py:54
  342.6 118.8 %collective-permute-start.2 = (bf16[1,2,1536,2560]{3,2,1,0:T(8,128)(2,1)}, bf16[1,2,1536,2560]{3,2,1,0:T(8,128)(2,1)}, u32[]{:S(2)}, u32[]{:S(2)}) collective-permute-start(bf16[1,2,1536,2560]{3,2,1,0:T(8,128)(2,1)} %get-tuple-element.12), channel_id=1, source_target_pairs={{0,0},{1,2},{2,4},{3,6},{4,1},{5,3},{6,5},{7,7}} | collective-permute-start | bytes 47185928 | tf_op jit(solution)/shard_map/ppermute | solution.py:54
  475.1 10.5 gather_fusion
  485.7 10.5 broadcast_select_fusion.1
  500.8 10.4 broadcast_in_dim.31
  511.2 13.2 constant_dynamic-update-slice_fusion.3
  524.4 642.0 %collective-permute-done.3 = bf16[1,2,1536,2560]{3,2,1,0:T(8,128)(2,1)} collective-permute-done((bf16[1,2,1536,2560]{3,2,1,0:T(8,128)(2,1)}, bf16[1,2,1536,2560]{3,2,1,0:T(8,128)(2,1)}, u32[]{:S(2)}, u32[]{:S(2)}) %collective-permute-start.3) | collective-permute-done | bytes 15728672 | tf_op jit(solution)/shard_map/ppermute | solution.py:54
  1166.4 13.2 constant_dynamic-update-slice_fusion.2
  1179.6 20.0 %broadcast_in_dim.30 = bf16[2,2,2560,3072]{3,2,1,0:T(8,128)(2,1)} broadcast(bf16[]{:T(256)} %constant.90.clone.1), dimensions={} | broadcast | bytes 62914560 | tf_op jit(solution)/shard_map/broadcast_in_dim | solution.py:48
  1199.6 21.4 %constant_dynamic-update-slice_fusion.5 = bf16[2,2,2560,3072]{3,2,1,0:T(8,128)(2,1)} fusion(bf16[2,2,2560,3072]{3,2,1,0:T(8,128)(2,1)} %broadcast_in_dim.30, bf16[1,2,2560,3072]{3,2,1,0:T(8,128)(2,1)} %collective-permute-done, s32[]{:T(128)S(6)} %select_n.86), kind=kLoop, calls=%fused_computation.97 | loop fusion | bytes 62914564 | tf_op jit(solution)/shard_map/dynamic_update_slice | solution.py:56
  1221.1 21.5 %constant_dynamic-update-slice_fusion.4 = bf16[2,2,2560,3072]{3,2,1,0:T(8,128)(2,1)} fusion(bf16[2,2,2560,3072]{3,2,1,0:T(8,128)(2,1)} %constant_dynamic-update-slice_fusion.5, bf16[1,2,2560,3072]{3,2,1,0:T(8,128)(2,1)} %collective-permute-done.1, s32[]{:T(128)S(6)} %select_n.90), kind=kLoop, calls=%fused_computation.95 | loop fusion | bytes 62914564 | tf_op jit(solution)/shard_map/dynamic_update_slice | solution.py:56
  1242.5 44.2 %fusion.8 = f32[8,2,144,3072]{3,2,0,1:T(8,128)} fusion(bf16[8,2,144,2560]{3,2,1,0:T(8,128)(2,1)} %all-to-all-done, bf16[2,2,2560,3072]{3,2,1,0:T(8,128)(2,1)} %constant_dynamic-update-slice_fusion.4), kind=kOutput, calls=%fused_computation.26 | convolution fusion | flops 36238786560 | bytes 71565312 | tf_op jit(solution)/shard_map/nxcd,xdg->nxcg/dot_general | solution.py:33
  1286.7 28.9 %convert_bitcast_fusion.1 = bf16[8,2,144,2560]{3,2,0,1:T(8,128)(2,1)} fusion(bf16[2,2,1536,2560]{3,2,1,0:T(8,128)(2,1)} %constant_dynamic-update-slice_fusion.2, f32[8,2,144,3072]{3,2,0,1:T(8,128)} %fusion.8), kind=kOutput, calls=%fused_computation.23 | convolution fusion | flops 18146525184 | bytes 55836672 | tf_op jit(solution)/shard_map/nxcf,xfd->nxcd/dot_general | solution.py:35
  1315.6 10.1 copy.46
  1343.2 117.2 %all-to-all-done.1 = bf16[8,2,144,2560]{3,2,1,0:T(8,128)(2,1)} async-done(((bf16[8,2,144,2560]{3,2,1,0:T(8,128)(2,1)}), bf16[8,2,144,2560]{3,2,1,0:T(8,128)(2,1)}, u32[]{:S(2)}, u32[]{:S(2)}) %all-to-all-start.1) | async-done | bytes 11796512 | tf_op jit(solution)/shard_map/all_to_all | solution.py:36
  1460.4 21.2 %gather_fusion.1 = bf16[1536,2560]{1,0:T(8,128)(2,1)} fusion(bf16[2304,2560]{1,0:T(8,128)(2,1)} %bitcast.11, s32[2048]{0:T(1024)S(1)} %pad_clamp_fusion.3), kind=kCustom, calls=%fused_computation.1.clone | custom fusion | bytes 15734784 | tf_op jit(solution)/shard_map/jit(_take)/gather | solution.py:37
  1481.6 9.8 select_convert_fusion.1
  1491.4 17.7 reshape.158
  1509.1 27.0 %multiply_reduce_fusion.1 = f32[256,2560]{1,0:T(8,128)S(1)} fusion(f32[256,6,2560]{2,1,0:T(8,128)} %reshape.158, f32[256,6]{1,0:T(8,128)S(1)} %bitcast.82), kind=kLoop, calls=%fused_computation.11 | loop fusion | flops 7208960 | bytes 18356224 | tf_op jit(solution)/shard_map/reduce_sum | solution.py:39
  1538.7 10.7 gather_fusion.2
  1556.0 133.3 %all_to_all.20 = bf16[8,2,144,2560]{3,2,1,0:T(8,128)(2,1)} all-to-all(bf16[8,2,144,2560]{3,2,1,0:T(8,128)(2,1)S(1)} %bitcast.81), channel_id=1, replica_groups=mesh['stage'=2,'expert'=4] {'stage','expert'}, dimensions={0} | all-to-all | bytes 23592960 | tf_op jit(solution)/shard_map/all_to_all | solution.py:32
  1689.3 44.2 %fusion.11 = f32[8,2,144,3072]{3,2,0,1:T(8,128)} fusion(bf16[8,2,144,2560]{3,2,1,0:T(8,128)(2,1)} %all_to_all.20, bf16[2,2,2560,3072]{3,2,1,0:T(8,128)(2,1)} %constant_dynamic-update-slice_fusion.4), kind=kOutput, calls=%fused_computation.27 | convolution fusion | flops 36238786560 | bytes 71565312 | tf_op jit(solution)/shard_map/nxcd,xdg->nxcg/dot_general | solution.py:33
  1733.5 28.7 %convert_bitcast_fusion = bf16[8,2,144,2560]{3,2,0,1:T(8,128)(2,1)} fusion(bf16[2,2,1536,2560]{3,2,1,0:T(8,128)(2,1)} %constant_dynamic-update-slice_fusion.2, f32[8,2,144,3072]{3,2,0,1:T(8,128)} %fusion.11), kind=kOutput, calls=%fused_computation.22 | convolution fusion | flops 18146525184 | bytes 55836672 | tf_op jit(solution)/shard_map/nxcf,xfd->nxcd/dot_general | solution.py:35
  1762.2 10.1 copy.54
  1776.8 130.4 %all-to-all-done.3 = bf16[8,2,144,2560]{3,2,1,0:T(8,128)(2,1)} async-done(((bf16[8,2,144,2560]{3,2,1,0:T(8,128)(2,1)}), bf16[8,2,144,2560]{3,2,1,0:T(8,128)(2,1)}, u32[]{:S(2)}, u32[]{:S(2)}) %all-to-all-start.3) | async-done | bytes 11796512 | tf_op jit(solution)/shard_map/all_to_all | solution.py:36
  1907.2 21.0 %gather_fusion.3 = bf16[1536,2560]{1,0:T(8,128)(2,1)} fusion(bf16[2304,2560]{1,0:T(8,128)(2,1)} %bitcast.24, s32[2048]{0:T(1024)S(1)} %pad_clamp_fusion.2), kind=kCustom, calls=%fused_computation.3.clone | custom fusion | bytes 15734784 | tf_op jit(solution)/shard_map/jit(_take)/gather | solution.py:37
  1937.9 17.7 reshape.159
  1955.7 27.0 %multiply_reduce_fusion = f32[256,2560]{1,0:T(8,128)S(1)} fusion(f32[256,6,2560]{2,1,0:T(8,128)} %reshape.159, f32[256,6]{1,0:T(8,128)S(1)} %bitcast.83), kind=kLoop, calls=%fused_computation.10 | loop fusion | flops 7208960 | bytes 18356224 | tf_op jit(solution)/shard_map/reduce_sum | solution.py:39
  (105 shorter events, 62.2 us)
Async XLA Ops:
  84.9 1094.7 %collective-permute-start = (bf16[1,2,2560,3072]{3,2,1,0:T(8,128)(2,1)}, bf16[1,2,2560,3072]{3,2,1,0:T(8,128)(2,1)}, u32[]{:S(2)}, u32[]{:S(2)}) collective-permute-start(bf16[1,2,2560,3072]{3,2,1,0:T(8,128)(2,1)} %get-tuple-element.10), channel_id=1, source_target_pairs={{0,0},{1,2},{2,4},{3,6},{4,1},{5,3},{6,5},{7,7}} | collective-permute-start | bytes 94371848 | tf_op jit(solution)/shard_map/ppermute | solution.py:53
  320.9 140.6 %copy-start.18 = (s32[2,256,6]{1,0,2:T(2,128)S(1)}, s32[2,256,6]{1,0,2:T(2,128)}, u32[]{:S(2)}) copy-start(s32[2,256,6]{1,0,2:T(2,128)} %param.14) | copy-start | bytes 36868
  320.9 153.6 %copy-start.2 = (bf16[256,2560]{1,0:T(8,128)(2,1)S(1)}, bf16[256,2560]{1,0:T(8,128)(2,1)}, u32[]{:S(2)}) copy-start(bf16[256,2560]{1,0:T(8,128)(2,1)} %param.13) | copy-start | bytes 3932164
  320.9 900.2 %collective-permute-start.1 = (bf16[1,2,2560,3072]{3,2,1,0:T(8,128)(2,1)}, bf16[1,2,2560,3072]{3,2,1,0:T(8,128)(2,1)}, u32[]{:S(2)}, u32[]{:S(2)}) collective-permute-start(bf16[1,2,2560,3072]{3,2,1,0:T(8,128)(2,1)} %get-tuple-element.9), channel_id=1, source_target_pairs={{0,1},{1,3},{2,5},{3,7},{4,0},{5,2},{6,4},{7,6}} | collective-permute-start | bytes 94371848 | tf_op jit(solution)/shard_map/ppermute | solution.py:53
  342.6 158.1 %collective-permute-start.2 = (bf16[1,2,1536,2560]{3,2,1,0:T(8,128)(2,1)}, bf16[1,2,1536,2560]{3,2,1,0:T(8,128)(2,1)}, u32[]{:S(2)}, u32[]{:S(2)}) collective-permute-start(bf16[1,2,1536,2560]{3,2,1,0:T(8,128)(2,1)} %get-tuple-element.12), channel_id=1, source_target_pairs={{0,0},{1,2},{2,4},{3,6},{4,1},{5,3},{6,5},{7,7}} | collective-permute-start | bytes 47185928 | tf_op jit(solution)/shard_map/ppermute | solution.py:54
  461.4 705.0 %collective-permute-start.3 = (bf16[1,2,1536,2560]{3,2,1,0:T(8,128)(2,1)}, bf16[1,2,1536,2560]{3,2,1,0:T(8,128)(2,1)}, u32[]{:S(2)}, u32[]{:S(2)}) collective-permute-start(bf16[1,2,1536,2560]{3,2,1,0:T(8,128)(2,1)} %get-tuple-element.11), channel_id=1, source_target_pairs={{0,1},{1,3},{2,5},{3,7},{4,0},{5,2},{6,4},{7,6}} | collective-permute-start | bytes 47185928 | tf_op jit(solution)/shard_map/ppermute | solution.py:54
  461.5 6.6 copy-start.14
  461.9 12.9 copy-start.6
  468.0 6.8 copy-start.20
  468.2 6.7 copy-start.10
  496.2 746.4 %all-to-all-start = ((bf16[8,2,144,2560]{3,2,1,0:T(8,128)(2,1)}), bf16[8,2,144,2560]{3,2,1,0:T(8,128)(2,1)}, u32[]{:S(2)}, u32[]{:S(2)}) async-start(bf16[8,2,144,2560]{3,2,1,0:T(8,128)(2,1)} %bitcast.80), calls=%async_computation | async-start | bytes 23592960 | tf_op jit(solution)/shard_map/all_to_all | solution.py:32
  1325.6 4.2 copy-start.15
  1325.6 4.6 copy-start.19
  1325.6 10.6 copy-start.16
  1325.7 17.4 copy-start.7
  1325.7 17.4 copy-start.11
  1325.7 134.7 %all-to-all-start.1 = ((bf16[8,2,144,2560]{3,2,1,0:T(8,128)(2,1)}), bf16[8,2,144,2560]{3,2,1,0:T(8,128)(2,1)}, u32[]{:S(2)}, u32[]{:S(2)}) async-start(bf16[8,2,144,2560]{3,2,1,0:T(8,128)(2,1)} %copy.46), calls=%async_computation.1 | async-start | bytes 23592960 | tf_op jit(solution)/shard_map/all_to_all | solution.py:36
  1330.3 151.3 %copy-start.8 = (s32[1536]{0:T(1024)}, s32[1536]{0:T(1024)S(1)}, u32[]{:S(2)}) copy-start(s32[1536]{0:T(1024)S(1)} %eq.65) | copy-start | bytes 18436
  1336.7 144.9 %copy-start.12 = (s32[1536]{0:T(1024)}, s32[1536]{0:T(1024)S(1)}, u32[]{:S(2)}) copy-start(s32[1536]{0:T(1024)S(1)} %fusion.24) | copy-start | bytes 18436
  1509.1 27.0 %copy-start.3 = (bf16[256,2560]{1,0:T(8,128)(2,1)S(1)}, bf16[256,2560]{1,0:T(8,128)(2,1)}, u32[]{:S(2)}) copy-start(bf16[256,2560]{1,0:T(8,128)(2,1)} %param.13) | copy-start | bytes 3932164
  1536.1 2.3 copy-start
  1772.3 4.3 copy-start.17
  1772.3 4.5 copy-start.9
  1772.3 4.5 copy-start.13
  1772.3 134.9 %all-to-all-start.3 = ((bf16[8,2,144,2560]{3,2,1,0:T(8,128)(2,1)}), bf16[8,2,144,2560]{3,2,1,0:T(8,128)(2,1)}, u32[]{:S(2)}, u32[]{:S(2)}) async-start(bf16[8,2,144,2560]{3,2,1,0:T(8,128)(2,1)} %copy.54), calls=%async_computation.3 | async-start | bytes 23592960 | tf_op jit(solution)/shard_map/all_to_all | solution.py:36
  1955.6 27.0 %copy-start.1 = (f32[256,2560]{1,0:T(8,128)S(1)}, f32[256,2560]{1,0:T(8,128)}, u32[]{:S(2)}) copy-start(f32[256,2560]{1,0:T(8,128)} %copy-done) | copy-start | bytes 7864324
  1955.6 27.1 %copy-start.4 = (bf16[256,2560]{1,0:T(8,128)(2,1)S(1)}, bf16[256,2560]{1,0:T(8,128)(2,1)}, u32[]{:S(2)}) copy-start(bf16[256,2560]{1,0:T(8,128)(2,1)} %param.13) | copy-start | bytes 3932164
  1955.7 27.6 %copy-start.5 = (f32[1,256,2560]{2,1,0:T(8,128)S(1)}, f32[1,256,2560]{2,1,0:T(8,128)}, u32[]{:S(2)}) copy-start(f32[1,256,2560]{2,1,0:T(8,128)} %get-tuple-element.13) | copy-start | bytes 7864324
where the time goes:
time: 2020 us; the launch traced here: 1990 us
  waiting for transfers between devices  890 us (44%)
  starting transfers between devices  368 us (18%)
  local copies, waits for them, and re-layouts  341 us (17%)
  matrix products  146 us (7%)
  blocking collectives  133 us (7%)
  other arithmetic  107 us (5%)
    ppermute x2, waiting for transfers between devices, hand_over(): lax.ppermute(lax.dynamic_slice_in_dim(down_loc, piece_idx * exp_dev, exp_...  642 us
    all_to_all x2, waiting for transfers between devices, moe_layer(): returned = lax.all_to_all(expert_out, FLAT, 0, 0, tiled=True)  248 us
    ppermute x2, starting transfers between devices, hand_over(): lax.ppermute(lax.dynamic_slice_in_dim(fused_loc, piece_idx * exp_dev, exp...  236 us
    all_to_all x1, blocking collectives, moe_layer(): inbound = lax.all_to_all(outbound, FLAT, 0, 0, tiled=True)  133 us
    ppermute x2, starting transfers between devices, hand_over(): lax.ppermute(lax.dynamic_slice_in_dim(down_loc, piece_idx * exp_dev, exp_...  119 us
    dot_general x2, matrix products, moe_layer(): jnp.einsum('nxcd,xdg->nxcg', inbound, layer_w13, preferred_element_type=j...  88.3 us
    dot_general x2, matrix products, moe_layer(): jnp.einsum('nxcf,xfd->nxcd', activated, layer_down, preferred_element_typ...  57.6 us
    reduce_sum x2, other arithmetic, moe_layer(): return hidden + jnp.sum(layer_mix[..., None] * picked, axis=1)  54 us
  transfers between devices with their start and end apart: 7, of which 3 were waited for; matrix products, arithmetic and copies ran while one was open for 9% of the time, Pallas kernels for 0%

commit v1 on v0

v1 whole, which is shorter than its diff:
```python
import functools

import jax
import jax.numpy as jnp
from jax import lax
from jax.experimental import pallas as pl
from jax.experimental.pallas import tpu as pltpu
from jax.sharding import PartitionSpec as P


NORM_EPS = 1e-6
FLAT = ("stage", "expert")
W13_CHUNKS = 4
DOWN_CHUNKS = 2


def norm_rows(hidden):
    return (hidden * lax.rsqrt(jnp.mean(hidden * hidden, axis=-1, keepdims=True) + NORM_EPS)).astype(jnp.bfloat16)


def copy_through(moves):
    for loads, _ in moves:
        for cp in loads:
            cp.start()
    for loads, store in moves:
        for cp in loads:
            cp.wait()
        store.start()
    for _, store in moves:
        store.wait()


def pick_w13_body(row_start, n, meta_ref, gate_ref, up_ref, out_ref, buf, sem_in, sem_out):
    exp_dev, rows, width = out_ref.shape
    half = width // 2
    tile = rows // n
    moves = []
    for e in range(exp_dev):
        for i in range(n):
            k = e * n + i
            src = pl.ds(row_start + i * tile, tile)
            exp = meta_ref[2] * exp_dev + e
            loads = [pltpu.make_async_copy(gate_ref.at[exp, src], buf.at[k, :, pl.ds(0, half)], sem_in.at[k, 0]),
                     pltpu.make_async_copy(up_ref.at[exp, src], buf.at[k, :, pl.ds(half, half)], sem_in.at[k, 1])]
            moves.append((loads, pltpu.make_async_copy(buf.at[k], out_ref.at[e, pl.ds(i * tile, tile)], sem_out.at[k])))
    copy_through(moves)


def pick_down_body(row_start, n, meta_ref, down_ref, out_ref, buf, sem_in, sem_out):
    exp_dev, rows, _ = out_ref.shape
    tile = rows // n
    moves = []
    for e in range(exp_dev):
        for i in range(n):
            k = e * n + i
            src = pl.ds(row_start + i * tile, tile)
            loads = [pltpu.make_async_copy(down_ref.at[meta_ref[2] * exp_dev + e, src], buf.at[k], sem_in.at[k, 0])]
            moves.append((loads, pltpu.make_async_copy(buf.at[k], out_ref.at[e, pl.ds(i * tile, tile)], sem_out.at[k])))
    copy_through(moves)


def place_body(row_start, n, meta_ref, landed_ref, own_ref, *rest):
    out_ref, buf, sem_in, sem_out = rest[-4:]
    exp_dev, rows, _ = landed_ref.shape
    tile = rows // n

    def moves_from(src_ref):
        moves = []
        for e in range(exp_dev):
            for i in range(n):
                k = e * n + i
                loads = [pltpu.make_async_copy(src_ref.at[e, pl.ds(i * tile, tile)], buf.at[k], sem_in.at[k])]
                moves.append((loads, pltpu.make_async_copy(buf.at[k], out_ref.at[meta_ref[0], e, pl.ds(row_start + i * tile, tile)], sem_out.at[k])))
        return moves

    pl.when(meta_ref[1] == 0)(lambda: copy_through(moves_from(landed_ref)))
    pl.when(meta_ref[1] != 0)(lambda: copy_through(moves_from(own_ref)))


HBM_SPEC = pl.BlockSpec(memory_space=pl.ANY)
SMEM_SPEC = pl.BlockSpec(memory_space=pltpu.SMEM)
COPY_COST = pl.CostEstimate(flops=5_000_000_000, bytes_accessed=16_000_000, transcendentals=0)
PIECES = 2


def pick(body, meta, sources, exp_dev, row_start, rows, width):
    dtype = sources[0].dtype
    n = PIECES
    return pl.pallas_call(
        functools.partial(body, row_start, n),
        out_shape=jax.ShapeDtypeStruct((exp_dev, rows, width), dtype),
        in_specs=[SMEM_SPEC] + [HBM_SPEC] * len(sources),
        out_specs=HBM_SPEC,
        scratch_shapes=[pltpu.VMEM((exp_dev * n, rows // n, width), dtype), pltpu.SemaphoreType.DMA((exp_dev * n, 2)), pltpu.SemaphoreType.DMA((exp_dev * n,))],
        cost_estimate=COPY_COST,
    )(meta, *sources)


def place(buffer, landed, own, meta, out_shape, row_start):
    exp_dev, rows, width = landed.shape
    n = PIECES
    args = [meta, landed, own] + ([] if buffer is None else [buffer])
    return pl.pallas_call(
        functools.partial(place_body, row_start, n),
        out_shape=jax.ShapeDtypeStruct(out_shape, landed.dtype),
        in_specs=[SMEM_SPEC] + [HBM_SPEC] * (len(args) - 1),
        out_specs=HBM_SPEC,
        scratch_shapes=[pltpu.VMEM((exp_dev * n, rows // n, width), landed.dtype), pltpu.SemaphoreType.DMA((exp_dev * n,)), pltpu.SemaphoreType.DMA((exp_dev * n,))],
        input_output_aliases={} if buffer is None else {3: 0},
        cost_estimate=COPY_COST,
    )(*args)


def round_meta(round_idx, n_stage, n_group):
    stage_idx = lax.axis_index("stage")
    group = lax.axis_index("expert")
    flat_idx = stage_idx * n_group + group
    piece = (stage_idx + round_idx) % n_stage
    is_self = group * n_stage + piece == flat_idx
    return jnp.stack([(flat_idx % n_stage - round_idx) % n_stage, is_self.astype(jnp.int32), piece]).astype(jnp.int32)


def send_round(round_idx, meta, gate_loc, up_loc, down_loc, n_stage, n_group):
    exp_dev = gate_loc.shape[0] // n_stage
    model_width, expert_width = gate_loc.shape[1:]
    pairs = [(s * n_group + g, g * n_stage + (s + round_idx) % n_stage) for s in range(n_stage) for g in range(n_group)]
    pairs = [p for p in pairs if p[0] != p[1]]
    chunks = []
    for kind, total, parts, width, body, sources in (
        ("w13", model_width, W13_CHUNKS, 2 * expert_width, pick_w13_body, (gate_loc, up_loc)),
        ("down", expert_width, DOWN_CHUNKS, model_width, pick_down_body, (down_loc,)),
    ):
        rows = total // parts
        for c in range(parts):
            idx = round_idx * (W13_CHUNKS + DOWN_CHUNKS) + len(chunks)
            own = pick(body, meta, sources, exp_dev, c * rows, rows, width)
            landed = lax.ppermute(own, FLAT, pairs)
            chunks.append((idx, kind, c * rows, own, landed))
    return chunks


def moe_body(layer_idx, dims, u_ref, mix_ref, gate_ref, up_ref, down_ref, parts_ref, stage_ref, tok, gbuf, ubuf, dbuf, act, acc, xbuf, xown, wcol, ld_sem, out_sem, g_sem, u_sem, d_sem, own_ss, own_rs, tok_ss, tok_rs, x_ss, x_rs, sum_ss, parts_rs):
    n_group, rows, width, ff, n_exp = dims
    block = 2 * rows
    g_tile = gbuf.shape[2]
    d_tile = dbuf.shape[2]
    g_steps = ff // g_tile
    d_steps = width // d_tile
    last = 2 * n_group - 1
    flat = lax.axis_index("stage") * n_group + lax.axis_index("expert")
    role = flat if layer_idx == 0 else last - flat
    chip = role // 2
    core = role % 2
    partner_role = 2 * chip + 1 - core

    def device(r):
        f = r if layer_idx == 0 else last - r
        return (f // n_group, f % n_group)

    def remote(src, dst, ss, rs, target):
        return pltpu.make_async_remote_copy(src_ref=src, dst_ref=dst, send_sem=ss, recv_sem=rs, device_id=device(target), device_id_type=pl.DeviceIdType.MESH)

    def tok_copy(b, target, kind):
        return remote(tok.at[b], tok.at[b], tok_ss.at[kind, b], tok_rs.at[b], target)

    def on(r, fn):
        pl.when(role == r)(fn)

    own_rows = pl.ds(pl.multiple_of(core * rows, rows), rows)
    other_rows = pl.ds(pl.multiple_of((1 - core) * rows, rows), rows)
    load_own = pltpu.make_async_copy(u_ref, tok.at[chip, own_rows], ld_sem)
    load_own.start()

    def g_copy(q):
        e, j, b = (q // g_steps) % n_exp, q % g_steps, q % 2
        cols = pl.ds(pl.multiple_of(j * g_tile, g_tile), g_tile)
        return (pltpu.make_async_copy(gate_ref.at[e, :, cols], gbuf.at[b], g_sem.at[b]),
                pltpu.make_async_copy(up_ref.at[e, :, cols], ubuf.at[b], u_sem.at[b]))

    def d_copy(p):
        e, n, b = (p // d_steps) % n_exp, p % d_steps, p % 2
        cols = pl.ds(pl.multiple_of(n * d_tile, d_tile), d_tile)
        return pltpu.make_async_copy(down_ref.at[e, :, cols], dbuf.at[b], d_sem.at[b])

    g_total = 4 * n_exp * g_steps
    d_total = 4 * n_exp * d_steps

    @pl.when(chip < 2)
    def _():
        for c in g_copy(0):
            c.start()
        d_copy(0).start()

    load_own.wait()
    own_copy = remote(tok.at[chip, own_rows], tok.at[chip, own_rows], own_ss, own_rs, partner_role)
    own_copy.start()
    own_copy.wait_recv()
    on(0, lambda: tok_copy(0, 2, 0).start())
    on(3, lambda: tok_copy(1, 1, 0).start())
    on(5, lambda: tok_copy(2, 0, 0).start())
    on(4, lambda: tok_copy(2, 3, 0).start())
    on(7, lambda: tok_copy(3, 1, 0).start())

    def x_copy(slot):
        return remote(acc.at[slot % 2], xbuf.at[slot % 2], x_ss.at[slot], x_rs.at[slot], partner_role)

    def own_x_copy():
        return remote(acc.at[0, other_rows], xown, x_ss.at[0], x_rs.at[0], partner_role)

    def reducer(slot):
        return {1: chip, 2: 1, 3: 0}[slot]

    def sum_copy(slot, h):
        b = {1: 1 - chip, 2: 2, 3: 3}[slot]
        return remote(stage_ref.at[slot - 1, pl.ds(h * rows, rows)], parts_ref.at[chip], sum_ss.at[slot - 1, h], parts_rs.at[chip], 2 * b + h)

    def give(slot):
        pl.when(core != reducer(slot))(lambda: x_copy(slot).start())

    def take(slot):
        @pl.when(core == reducer(slot))
        def _():
            x_copy(slot).wait_recv()
            s = slot % 2

            def add(i, carry):
                r = pl.ds(pl.multiple_of(i * 64, 64), 64)
                acc[s, r] = acc[s, r] + xbuf[s, r]
                return carry

            lax.fori_loop(0, block // 64, add, 0)
            store = pltpu.make_async_copy(acc.at[s], stage_ref.at[slot - 1], out_sem)
            store.start()
            store.wait()
            for h in range(2):
                sum_copy(slot, h).start()

        pl.when(core != reducer(slot))(lambda: x_copy(slot).wait_send())

    def forward(r_from, r_to, b, kind):
        @pl.when(role == r_from)
        def _():
            tok_copy(b, r_to, kind).wait_recv()
            tok_copy(b, r_to, kind).start()

    def arrive(r, b):
        on(r, lambda: tok_copy(b, r, 1).wait_recv())

    def experts(hs):
        slot = hs // 2
        s = slot % 2
        late = slot // 2
        blk = late * slot + (1 - late) * ((chip + slot) % 2)
        mix_rows = pl.ds(pl.multiple_of(blk * block, block), block)

        def one_expert(ee, carry):
            e = (hs % 2) * (n_exp // 2) + ee
            lane = lax.broadcasted_iota(jnp.int32, (block, 128), 1)
            col = jnp.sum(jnp.where(lane == e, mix_ref[mix_rows, :], 0.0), axis=1, keepdims=True)
            wcol[...] = jnp.broadcast_to(col, (block, 128))

            @pl.when(e == 0)
            def _():
                def clear(i, c):
                    r = pl.ds(pl.multiple_of(i * 64, 64), 64)
                    acc[s, r] = jnp.zeros((64, width), jnp.float32)
                    return c

                lax.fori_loop(0, block // 64, clear, 0)

            def up_step(j, c):
                q = (slot * n_exp + e) * g_steps + j
                b = q % 2
                for cp in g_copy(q):
                    cp.wait()

                @pl.when(q + 1 < g_total)
                def _():
                    for cp in g_copy(q + 1):
                        cp.start()

                def part(n, c2):
                    cols = pl.ds(pl.multiple_of(n * 256, 256), 256)
                    zg = jnp.dot(tok[blk], gbuf[b, :, cols], preferred_element_type=jnp.float32)
                    zu = jnp.dot(tok[blk], ubuf[b, :, cols], preferred_element_type=jnp.float32)
                    a = (zg * jax.nn.sigmoid(zg) * zu).astype(jnp.bfloat16)
                    act[:, pl.ds(pl.multiple_of(j * g_tile + n * 256, 256), 256)] = a
                    return c2

                return lax.fori_loop(0, g_tile // 256, part, c)

            lax.fori_loop(0, g_steps, up_step, 0)

            def down_step(n, c):
                p = (slot * n_exp + e) * d_steps + n
                b = p % 2
                d_copy(p).wait()

                @pl.when(p + 1 < d_total)
                def _():
                    d_copy(p + 1).start()

                def part(m, c2):
                    cols = pl.ds(pl.multiple_of(m * 256, 256), 256)
                    o = jnp.dot(act[...], dbuf[b, :, cols], preferred_element_type=jnp.float32).astype(jnp.bfloat16)
                    w = jnp.concatenate([wcol[...], wcol[...]], axis=1)
                    out_cols = pl.ds(pl.multiple_of(n * d_tile + m * 256, 256), 256)
                    acc[s, :, out_cols] = acc[s, :, out_cols] + jnp.where(w > 0, w * o.astype(jnp.float32), 0.0)
                    return c2

                return lax.fori_loop(0, d_tile // 256, part, c)

            lax.fori_loop(0, d_steps, down_step, 0)
            return carry

        lax.fori_loop(0, n_exp // 2, one_expert, 0)

    @pl.when(chip < 2)
    def _():
        def half(hs, carry):
            @pl.when(hs == 2)
            def _():
                own_x_copy().start()
                forward(1, 0, 1, 1)
                forward(2, 3, 0, 1)
                arrive(0, 1)
                arrive(3, 0)

            @pl.when(hs == 3)
            def _():
                own_x_copy().wait_recv()

                def add(i, c):
                    r = pl.ds(pl.multiple_of(core * rows + i * 64, 64), 64)
                    acc[0, r] = acc[0, r] + xown[pl.ds(pl.multiple_of(i * 64, 64), 64)]
                    return c

                lax.fori_loop(0, rows // 64, add, 0)
                store = pltpu.make_async_copy(acc.at[0, own_rows], parts_ref.at[chip], out_sem)
                store.start()
                store.wait()
                own_x_copy().wait_send()
                forward(0, 1, 2, 1)
                forward(3, 2, 2, 1)
                forward(1, 0, 3, 1)
                forward(0, 2, 3, 0)

            @pl.when(hs == 4)
            def _():
                give(1)
                arrive(1, 2)
                arrive(2, 2)

            @pl.when(hs == 5)
            def _():
                take(1)
                forward(2, 3, 3, 1)

            @pl.when(hs == 6)
            def _():
                give(2)
                arrive(3, 3)

            pl.when(hs == 7)(lambda: take(2))
            experts(hs)
            return carry

        lax.fori_loop(0, 8, half, 0)
        give(3)
        take(3)
        for slot in (1, 2, 3):
            @pl.when(core == reducer(slot))
            def _():
                for h in range(2):
                    sum_copy(slot, h).wait_send()

    own_copy.wait_send()
    for r, b, target, kind in ((0, 0, 2, 0), (3, 1, 1, 0), (5, 2, 0, 0), (4, 2, 3, 0), (7, 3, 1, 0), (1, 1, 0, 1), (2, 0, 3, 1), (0, 2, 1, 1), (3, 2, 2, 1), (1, 3, 0, 1), (0, 3, 2, 0), (2, 3, 3, 1)):
        on(r, lambda: tok_copy(b, target, kind).wait_send())
    for k in range(2):
        @pl.when(chip != k)
        def _():
            remote(parts_ref.at[k], parts_ref.at[k], sum_ss.at[0, 0], parts_rs.at[k], partner_role).wait_recv()


def moe_layer(layer_idx, n_group, tokens, mix, gate_w, up_w, down_w):
    rows, width = tokens.shape
    n_exp, _, ff = gate_w.shape
    block = 2 * rows
    hbm = pl.BlockSpec(memory_space=pl.ANY)
    dma = pltpu.SemaphoreType.DMA
    g_tile, d_tile = ff // 3, width // 2
    flops = 2 * 8 * rows * n_exp * 3 * width * ff
    parts, _ = pl.pallas_call(
        functools.partial(moe_body, layer_idx, (n_group, rows, width, ff, n_exp)),
        out_shape=(jax.ShapeDtypeStruct((2, rows, width), jnp.float32), jax.ShapeDtypeStruct((3, block, width), jnp.float32)),
        in_specs=[hbm, pl.BlockSpec(memory_space=pltpu.VMEM), hbm, hbm, hbm],
        out_specs=(hbm, hbm),
        scratch_shapes=[
            pltpu.VMEM((4, block, width), jnp.bfloat16),
            pltpu.VMEM((2, width, g_tile), jnp.bfloat16),
            pltpu.VMEM((2, width, g_tile), jnp.bfloat16),
            pltpu.VMEM((2, ff, d_tile), jnp.bfloat16),
            pltpu.VMEM((block, ff), jnp.bfloat16),
            pltpu.VMEM((2, block, width), jnp.float32),
            pltpu.VMEM((2, block, width), jnp.float32),
            pltpu.VMEM((rows, width), jnp.float32),
            pltpu.VMEM((block, 128), jnp.float32),
            dma, dma, dma((2,)), dma((2,)), dma((2,)), dma, dma, dma((2, 4)), dma((4,)), dma((4,)), dma((4,)), dma((3, 2)), dma((2,)),
        ],
        compiler_params=pltpu.CompilerParams(has_side_effects=True, vmem_limit_bytes=64 * 1000 * 1000),
        cost_estimate=pl.CostEstimate(flops=flops, bytes_accessed=4 * 3 * n_exp * width * ff * 2, transcendentals=0),
    )(tokens, mix, gate_w, up_w, down_w)
    return parts


def solution(mesh):
    n_stage = mesh.shape["stage"]
    n_group = mesh.shape["expert"]

    def per_device(gate_loc, up_loc, down_loc, x_loc, ids_loc, mix_loc):
        group_idx = lax.axis_index("expert")
        weights = (gate_loc[0], up_loc[0], down_loc[0])
        exp_loc = gate_loc.shape[1]
        exp_dev = exp_loc // n_stage
        n_experts = exp_loc * n_group
        chosen = ids_loc[..., None] == jnp.arange(n_experts)[None, None, None, :]
        dense_mix = jnp.sum(jnp.where(chosen, mix_loc[..., None], 0.0), axis=2)
        all_mix = lax.all_gather(dense_mix, FLAT, axis=0)
        hidden = x_loc.astype(jnp.float32)
        normed = norm_rows(hidden)
        chunks = []
        layer_outs = []
        for layer_idx in range(n_stage):
            meta = round_meta(layer_idx, n_stage, n_group)
            meta, all_mix, normed = lax.optimization_barrier((meta, all_mix, normed))
            chunks += send_round(layer_idx, meta, *weights, n_stage, n_group)
            layer_mix = all_mix[:, layer_idx]
            layer_mix = layer_mix[::-1] if layer_idx else layer_mix
            mine = lax.dynamic_slice_in_dim(layer_mix.reshape(-1, n_experts), group_idx * exp_loc, exp_loc, axis=1)
            mine = jnp.pad(mine, ((0, 0), (0, 128 - exp_loc)))
            parts = moe_layer(layer_idx, n_group, normed, mine, *weights)
            hidden = hidden + (parts[0] + parts[1])
            normed = norm_rows(hidden)
            layer_outs.append(hidden)
        outs = {"w13": None, "down": None}
        shapes = {"w13": (n_stage, exp_dev, gate_loc.shape[2], 2 * gate_loc.shape[3]), "down": (n_stage, exp_dev) + down_loc.shape[2:]}
        metas = [round_meta(r, n_stage, n_group) for r in range(n_stage)]
        for idx, kind, row_start, own, landed in chunks:
            outs[kind] = place(outs[kind], landed, own, metas[idx // (len(chunks) // n_stage)], shapes[kind], row_start)
        return outs["w13"], outs["down"], jnp.stack(layer_outs)

    weight_spec = P("stage", "expert")
    token_spec = P(None, FLAT)
    return jax.shard_map(per_device, mesh=mesh, in_specs=(weight_spec, weight_spec, weight_spec, P(FLAT), token_spec, token_spec), out_specs=(token_spec, token_spec, token_spec), check_vma=False)
```

time: 2020 us -> 1490 us (0.74)
  the two profiles are of different devices: /device:TPU:0 before, /device:TPU:2 now
where the time goes in v1:
time: 1490 us
  Pallas kernels  1180 us (79%)
  waiting for transfers between devices  192 us (13%)
  starting transfers between devices  79.4 us (5%)
  other arithmetic  16 us (1%)
    pallas_call x2, Pallas kernels, moe_layer(): pl.pallas_call(functools.partial(moe_body, layer_idx, (n_group, rows, wid...  1010 us
    ppermute x12, waiting for transfers between devices, send_round(): landed = lax.ppermute(own, FLAT, pairs)  192 us
    pallas_call x12, Pallas kernels, pick(): pl.pallas_call(functools.partial(body, row_start, n), out_shape=jax.Shape...  87.9 us
    pallas_call x12, Pallas kernels, place(): pl.pallas_call(functools.partial(place_body, row_start, n), out_shape=jax...  86.3 us
    ppermute x12, starting transfers between devices, send_round(): landed = lax.ppermute(own, FLAT, pairs)  79.4 us
  transfers between devices with their start and end apart: 12, of which 3 were waited for; matrix products, arithmetic and copies ran while one was open for 1% of the time, Pallas kernels for 78%

profile of v1, /device:TPU:2, one launch (start us, length us, event | category | flops | bytes accessed | tf_op | source)
XLA Modules:
  0.0 1487.2 jit_solution(10351845556697530733)
XLA Ops:
  6.4 11.6 all-gather
  18.7 7.3 shard_map.93.own_ref
  29.4 7.3 shard_map.92.own_ref
  38.7 7.3 shard_map.91.own_ref
  46.0 3.6 collective-permute-start.5
  49.7 7.4 shard_map.90.own_ref
  62.2 417.8 %shard_map.85 = (f32[2,256,2560]{2,1,0:T(8,128)}, f32[3,512,2560]{2,1,0:T(8,128)}) custom-call(bf16[256,2560]{1,0:T(8,128)(2,1)} %fusion.1.u_ref, f32[2048,128]{1,0:T(8,128)} %pad.7.mix_ref, bf16[4,2560,1536]{2,1,0:T(8,128)(2,1)} %bitcast.28, bf16[4,2560,1536]{2,1,0:T(8,128)(2,1)} %bitcast.38, bf16[4,1536,2560]{2,1,0:T(8,128)(2,1)} %bitcast.44), custom_call_target="tpu_custom_call" | custom-call | flops 193273528320 | bytes 377487360 | tf_op jit(solution)/shard_map/pallas_call | solution.py:394
  486.5 7.3 shard_map.89.own_ref
  493.9 57.8 %collective-permute-start.3 = (bf16[2,640,3072]{2,1,0:T(8,128)(2,1)}, bf16[2,640,3072]{2,1,0:T(8,128)(2,1)}, u32[]{:S(2)}, u32[]{:S(2)}) collective-permute-start(bf16[2,640,3072]{2,1,0:T(8,128)(2,1)} %shard_map.89.own_ref), channel_id=1, source_target_pairs={{0,1},{1,3},{2,5},{3,7},{4,0},{5,2},{6,4},{7,6}} | collective-permute-start | bytes 23592968 | tf_op jit(solution)/shard_map/ppermute | solution.py:137
  551.7 7.4 shard_map.88.own_ref
  559.1 7.5 shard_map.105.own_ref
  570.4 7.3 shard_map.87.own_ref
  577.7 7.3 shard_map.86.own_ref
  585.0 7.3 shard_map.104.own_ref
  592.3 7.3 shard_map.103.own_ref
  599.6 7.2 shard_map.102.own_ref
  609.5 28.0 %collective-permute-done.3.landed_ref = bf16[2,640,3072]{2,1,0:T(8,128)(2,1)} collective-permute-done((bf16[2,640,3072]{2,1,0:T(8,128)(2,1)}, bf16[2,640,3072]{2,1,0:T(8,128)(2,1)}, u32[]{:S(2)}, u32[]{:S(2)}) %collective-permute-start.3) | collective-permute-done | bytes 7864352 | tf_op jit(solution)/shard_map/ppermute | solution.py:137
  639.5 82.3 %collective-permute-done.2.landed_ref = bf16[2,640,3072]{2,1,0:T(8,128)(2,1)} collective-permute-done((bf16[2,640,3072]{2,1,0:T(8,128)(2,1)}, bf16[2,640,3072]{2,1,0:T(8,128)(2,1)}, u32[]{:S(2)}, u32[]{:S(2)}) %collective-permute-start.2) | collective-permute-done | bytes 7864352 | tf_op jit(solution)/shard_map/ppermute | solution.py:137
  724.4 81.5 %collective-permute-done.11.landed_ref = bf16[2,768,2560]{2,1,0:T(8,128)(2,1)} collective-permute-done((bf16[2,768,2560]{2,1,0:T(8,128)(2,1)}, bf16[2,768,2560]{2,1,0:T(8,128)(2,1)}, u32[]{:S(2)}, u32[]{:S(2)}) %collective-permute-start.11) | collective-permute-done | bytes 7864352 | tf_op jit(solution)/shard_map/ppermute | solution.py:137
  805.9 588.9 %shard_map.110 = (f32[2,256,2560]{2,1,0:T(8,128)}, f32[3,512,2560]{2,1,0:T(8,128)}) custom-call(bf16[256,2560]{1,0:T(8,128)(2,1)} %multiply_convert_fusion.u_ref, f32[2048,128]{1,0:T(8,128)} %pad.8.mix_ref, bf16[4,2560,1536]{2,1,0:T(8,128)(2,1)} %bitcast.33, bf16[4,2560,1536]{2,1,0:T(8,128)(2,1)} %bitcast.43, bf16[4,1536,2560]{2,1,0:T(8,128)(2,1)} %bitcast.49), custom_call_target="tpu_custom_call" | custom-call | flops 193273528320 | bytes 377487360 | tf_op jit(solution)/shard_map/pallas_call | solution.py:394
  1400.8 7.2 shard_map.94.rest_0_
  1408.0 7.2 shard_map.106.rest_0_
  1415.2 7.2 shard_map.95.rest_0_
  1422.4 7.2 shard_map.96.rest_0_
  1429.6 7.2 shard_map.97.rest_0_
  1436.8 7.2 shard_map.98.rest_0_
  1444.0 7.2 shard_map.99.rest_0_
  1451.2 7.2 shard_map.100.rest_0_
  1458.4 7.2 shard_map.101
  1465.6 7.2 shard_map.107.rest_0_
  1472.8 7.2 shard_map.108.rest_0_
  1480.0 7.2 shard_map.109
  (51 shorter events, 40.3 us)
Async XLA Ops:
  18.1 42.4 %copy-start.3 = (f32[16,256,16]{1,2,0:T(8,128)}, f32[16,256,16]{1,2,0:T(8,128)S(1)}, u32[]{:S(2)}) copy-start(f32[16,256,16]{1,2,0:T(8,128)S(1)} %all-gather) | copy-start | bytes 786436
  26.0 540.5 %collective-permute-start.7 = (bf16[2,640,3072]{2,1,0:T(8,128)(2,1)}, bf16[2,640,3072]{2,1,0:T(8,128)(2,1)}, u32[]{:S(2)}, u32[]{:S(2)}) collective-permute-start(bf16[2,640,3072]{2,1,0:T(8,128)(2,1)} %shard_map.93.own_ref), channel_id=1, source_target_pairs={{1,2},{2,4},{3,6},{4,1},{5,3},{6,5}} | collective-permute-start | bytes 23592968 | tf_op jit(solution)/shard_map/ppermute | solution.py:137
  36.8 529.8 %collective-permute-start.6 = (bf16[2,640,3072]{2,1,0:T(8,128)(2,1)}, bf16[2,640,3072]{2,1,0:T(8,128)(2,1)}, u32[]{:S(2)}, u32[]{:S(2)}) collective-permute-start(bf16[2,640,3072]{2,1,0:T(8,128)(2,1)} %shard_map.92.own_ref), channel_id=1, source_target_pairs={{1,2},{2,4},{3,6},{4,1},{5,3},{6,5}} | collective-permute-start | bytes 23592968 | tf_op jit(solution)/shard_map/ppermute | solution.py:137
  46.0 560.8 %collective-permute-start.5 = (bf16[2,640,3072]{2,1,0:T(8,128)(2,1)}, bf16[2,640,3072]{2,1,0:T(8,128)(2,1)}, u32[]{:S(2)}, u32[]{:S(2)}) collective-permute-start(bf16[2,640,3072]{2,1,0:T(8,128)(2,1)} %shard_map.91.own_ref), channel_id=1, source_target_pairs={{1,2},{2,4},{3,6},{4,1},{5,3},{6,5}} | collective-permute-start | bytes 23592968 | tf_op jit(solution)/shard_map/ppermute | solution.py:137
  57.0 552.4 %collective-permute-start.4 = (bf16[2,640,3072]{2,1,0:T(8,128)(2,1)}, bf16[2,640,3072]{2,1,0:T(8,128)(2,1)}, u32[]{:S(2)}, u32[]{:S(2)}) collective-permute-start(bf16[2,640,3072]{2,1,0:T(8,128)(2,1)} %shard_map.90.own_ref), channel_id=1, source_target_pairs={{1,2},{2,4},{3,6},{4,1},{5,3},{6,5}} | collective-permute-start | bytes 23592968 | tf_op jit(solution)/shard_map/ppermute | solution.py:137
  62.2 418.5 %copy-start.2 = (bf16[256,2560]{1,0:T(8,128)(2,1)S(1)}, bf16[256,2560]{1,0:T(8,128)(2,1)}, u32[]{:S(2)}) copy-start(bf16[256,2560]{1,0:T(8,128)(2,1)} %param.9) | copy-start | bytes 3932164
  483.8 1.5 copy-start
  493.9 143.7 %collective-permute-start.3 = (bf16[2,640,3072]{2,1,0:T(8,128)(2,1)}, bf16[2,640,3072]{2,1,0:T(8,128)(2,1)}, u32[]{:S(2)}, u32[]{:S(2)}) collective-permute-start(bf16[2,640,3072]{2,1,0:T(8,128)(2,1)} %shard_map.89.own_ref), channel_id=1, source_target_pairs={{0,1},{1,3},{2,5},{3,7},{4,0},{5,2},{6,4},{7,6}} | collective-permute-start | bytes 23592968 | tf_op jit(solution)/shard_map/ppermute | solution.py:137
  559.1 9.5 copy-start.4
  566.6 155.2 %collective-permute-start.2 = (bf16[2,640,3072]{2,1,0:T(8,128)(2,1)}, bf16[2,640,3072]{2,1,0:T(8,128)(2,1)}, u32[]{:S(2)}, u32[]{:S(2)}) collective-permute-start(bf16[2,640,3072]{2,1,0:T(8,128)(2,1)} %shard_map.88.own_ref), channel_id=1, source_target_pairs={{0,1},{1,3},{2,5},{3,7},{4,0},{5,2},{6,4},{7,6}} | collective-permute-start | bytes 23592968 | tf_op jit(solution)/shard_map/ppermute | solution.py:137
  566.6 239.3 %collective-permute-start.11 = (bf16[2,768,2560]{2,1,0:T(8,128)(2,1)}, bf16[2,768,2560]{2,1,0:T(8,128)(2,1)}, u32[]{:S(2)}, u32[]{:S(2)}) collective-permute-start(bf16[2,768,2560]{2,1,0:T(8,128)(2,1)} %shard_map.105.own_ref), channel_id=1, source_target_pairs={{1,2},{2,4},{3,6},{4,1},{5,3},{6,5}} | collective-permute-start | bytes 23592968 | tf_op jit(solution)/shard_map/ppermute | solution.py:137
  606.8 844.4 %collective-permute-start.1 = (bf16[2,640,3072]{2,1,0:T(8,128)(2,1)}, bf16[2,640,3072]{2,1,0:T(8,128)(2,1)}, u32[]{:S(2)}, u32[]{:S(2)}) collective-permute-start(bf16[2,640,3072]{2,1,0:T(8,128)(2,1)} %shard_map.87.own_ref), channel_id=1, source_target_pairs={{0,1},{1,3},{2,5},{3,7},{4,0},{5,2},{6,4},{7,6}} | collective-permute-start | bytes 23592968 | tf_op jit(solution)/shard_map/ppermute | solution.py:137
  609.5 848.9 %collective-permute-start = (bf16[2,640,3072]{2,1,0:T(8,128)(2,1)}, bf16[2,640,3072]{2,1,0:T(8,128)(2,1)}, u32[]{:S(2)}, u32[]{:S(2)}) collective-permute-start(bf16[2,640,3072]{2,1,0:T(8,128)(2,1)} %shard_map.86.own_ref), channel_id=1, source_target_pairs={{0,1},{1,3},{2,5},{3,7},{4,0},{5,2},{6,4},{7,6}} | collective-permute-start | bytes 23592968 | tf_op jit(solution)/shard_map/ppermute | solution.py:137
  637.5 828.1 %collective-permute-start.10 = (bf16[2,768,2560]{2,1,0:T(8,128)(2,1)}, bf16[2,768,2560]{2,1,0:T(8,128)(2,1)}, u32[]{:S(2)}, u32[]{:S(2)}) collective-permute-start(bf16[2,768,2560]{2,1,0:T(8,128)(2,1)} %shard_map.104.own_ref), channel_id=1, source_target_pairs={{1,2},{2,4},{3,6},{4,1},{5,3},{6,5}} | collective-permute-start | bytes 23592968 | tf_op jit(solution)/shard_map/ppermute | solution.py:137
  721.8 751.0 %collective-permute-start.9 = (bf16[2,768,2560]{2,1,0:T(8,128)(2,1)}, bf16[2,768,2560]{2,1,0:T(8,128)(2,1)}, u32[]{:S(2)}, u32[]{:S(2)}) collective-permute-start(bf16[2,768,2560]{2,1,0:T(8,128)(2,1)} %shard_map.103.own_ref), channel_id=1, source_target_pairs={{0,1},{1,3},{2,5},{3,7},{4,0},{5,2},{6,4},{7,6}} | collective-permute-start | bytes 23592968 | tf_op jit(solution)/shard_map/ppermute | solution.py:137
  805.9 674.1 %collective-permute-start.8 = (bf16[2,768,2560]{2,1,0:T(8,128)(2,1)}, bf16[2,768,2560]{2,1,0:T(8,128)(2,1)}, u32[]{:S(2)}, u32[]{:S(2)}) collective-permute-start(bf16[2,768,2560]{2,1,0:T(8,128)(2,1)} %shard_map.102.own_ref), channel_id=1, source_target_pairs={{0,1},{1,3},{2,5},{3,7},{4,0},{5,2},{6,4},{7,6}} | collective-permute-start | bytes 23592968 | tf_op jit(solution)/shard_map/ppermute | solution.py:137
  805.9 588.9 %copy-start.1 = (f32[256,2560]{1,0:T(8,128)S(1)}, f32[256,2560]{1,0:T(8,128)}, u32[]{:S(2)}) copy-start(f32[256,2560]{1,0:T(8,128)} %copy-done) | copy-start | bytes 7864324

commit v2 on v1

--- a/solution.py
+++ b/solution.py
@@ -80,7 +80,7 @@
 HBM_SPEC = pl.BlockSpec(memory_space=pl.ANY)
 SMEM_SPEC = pl.BlockSpec(memory_space=pltpu.SMEM)
 COPY_COST = pl.CostEstimate(flops=5_000_000_000, bytes_accessed=16_000_000, transcendentals=0)
-PIECES = 2
+PIECES = 4
 
 
 def pick(body, meta, sources, exp_dev, row_start, rows, width):
@@ -139,7 +139,7 @@
     return chunks
 
 
-def moe_body(layer_idx, dims, u_ref, mix_ref, gate_ref, up_ref, down_ref, parts_ref, stage_ref, tok, gbuf, ubuf, dbuf, act, acc, xbuf, xown, wcol, ld_sem, out_sem, g_sem, u_sem, d_sem, own_ss, own_rs, tok_ss, tok_rs, x_ss, x_rs, sum_ss, parts_rs):
+def moe_body(layer_idx, dims, u_ref, mix_ref, gate_ref, up_ref, down_ref, parts_ref, stage_ref, tok, gbuf, ubuf, dbuf, act, acc, xbuf, xown, wcol, ld_sem, out_sem, g_sem, u_sem, d_sem, own_ss, own_rs, tok_ss, tok_rs, x_ss, x_rs, sum_ss, parts_rs, spare_ss, spare_rs):
     n_group, rows, width, ff, n_exp = dims
     block = 2 * rows
     g_tile = gbuf.shape[2]
@@ -208,11 +208,14 @@
         return remote(acc.at[0, other_rows], xown, x_ss.at[0], x_rs.at[0], partner_role)
 
     def reducer(slot):
-        return {1: chip, 2: 1, 3: 0}[slot]
+        return {1: 1, 2: chip, 3: 0}[slot]
 
     def sum_copy(slot, h):
-        b = {1: 1 - chip, 2: 2, 3: 3}[slot]
+        b = {1: 2, 2: 1 - chip, 3: 3}[slot]
         return remote(stage_ref.at[slot - 1, pl.ds(h * rows, rows)], parts_ref.at[chip], sum_ss.at[slot - 1, h], parts_rs.at[chip], 2 * b + h)
+
+    def spare_copy():
+        return remote(stage_ref.at[1, pl.ds(0, rows)], xbuf.at[0, pl.ds(0, rows)], spare_ss, spare_rs, 1)
 
     def give(slot):
         pl.when(core != reducer(slot))(lambda: x_copy(slot).start())
@@ -246,15 +249,14 @@
     def arrive(r, b):
         on(r, lambda: tok_copy(b, r, 1).wait_recv())
 
-    def experts(hs):
-        slot = hs // 2
+    def experts(step):
+        slot = step // n_exp
         s = slot % 2
-        late = slot // 2
-        blk = late * slot + (1 - late) * ((chip + slot) % 2)
+        blk = jnp.where(slot == 0, chip, jnp.where(slot == 1, 2, jnp.where(slot == 2, 1 - chip, 3)))
         mix_rows = pl.ds(pl.multiple_of(blk * block, block), block)
 
-        def one_expert(ee, carry):
-            e = (hs % 2) * (n_exp // 2) + ee
+        def one_expert():
+            e = step % n_exp
             lane = lax.broadcasted_iota(jnp.int32, (block, 128), 1)
             col = jnp.sum(jnp.where(lane == e, mix_ref[mix_rows, :], 0.0), axis=1, keepdims=True)
             wcol[...] = jnp.broadcast_to(col, (block, 128))
@@ -311,22 +313,21 @@
                 return lax.fori_loop(0, d_tile // 256, part, c)
 
             lax.fori_loop(0, d_steps, down_step, 0)
-            return carry
-
-        lax.fori_loop(0, n_exp // 2, one_expert, 0)
+
+        one_expert()
 
     @pl.when(chip < 2)
     def _():
-        def half(hs, carry):
-            @pl.when(hs == 2)
+        def step_body(step, carry):
+            @pl.when(step == n_exp)
             def _():
                 own_x_copy().start()
-                forward(1, 0, 1, 1)
-                forward(2, 3, 0, 1)
-                arrive(0, 1)
-                arrive(3, 0)
-
-            @pl.when(hs == 3)
+                forward(0, 1, 2, 1)
+                forward(3, 2, 2, 1)
+                arrive(1, 2)
+                arrive(2, 2)
+
+            @pl.when(step == n_exp + 1)
             def _():
                 own_x_copy().wait_recv()
 
@@ -340,34 +341,39 @@
                 store.start()
                 store.wait()
                 own_x_copy().wait_send()
-                forward(0, 1, 2, 1)
-                forward(3, 2, 2, 1)
+                forward(1, 0, 1, 1)
+                forward(2, 3, 0, 1)
                 forward(1, 0, 3, 1)
-                forward(0, 2, 3, 0)
-
-            @pl.when(hs == 4)
+
+            pl.when(step == n_exp + 2)(lambda: forward(0, 2, 3, 0))
+
+            @pl.when(step == 2 * n_exp)
             def _():
                 give(1)
-                arrive(1, 2)
-                arrive(2, 2)
-
-            @pl.when(hs == 5)
-            def _():
-                take(1)
-                forward(2, 3, 3, 1)
-
-            @pl.when(hs == 6)
+                arrive(0, 1)
+                arrive(3, 0)
+
+            pl.when(step == 2 * n_exp + 1)(lambda: take(1))
+            pl.when(step == 2 * n_exp + 2)(lambda: forward(2, 3, 3, 1))
+
+            @pl.when(step == 3 * n_exp)
             def _():
                 give(2)
                 arrive(3, 3)
 
-            pl.when(hs == 7)(lambda: take(2))
-            experts(hs)
+            @pl.when(step == 3 * n_exp + 1)
+            def _():
+                take(2)
+                on(3, lambda: spare_copy().start())
+
+            experts(step)
             return carry
 
-        lax.fori_loop(0, 8, half, 0)
+        lax.fori_loop(0, 4 * n_exp, step_body, 0)
         give(3)
         take(3)
+        on(3, lambda: spare_copy().wait_send())
+        on(1, lambda: spare_copy().wait_recv())
         for slot in (1, 2, 3):
             @pl.when(core == reducer(slot))
             def _():
@@ -406,7 +412,7 @@
             pltpu.VMEM((2, block, width), jnp.float32),
             pltpu.VMEM((rows, width), jnp.float32),
             pltpu.VMEM((block, 128), jnp.float32),
-            dma, dma, dma((2,)), dma((2,)), dma((2,)), dma, dma, dma((2, 4)), dma((4,)), dma((4,)), dma((4,)), dma((3, 2)), dma((2,)),
+            dma, dma, dma((2,)), dma((2,)), dma((2,)), dma, dma, dma((2, 4)), dma((4,)), dma((4,)), dma((4,)), dma((3, 2)), dma((2,)), dma, dma,
         ],
         compiler_params=pltpu.CompilerParams(has_side_effects=True, vmem_limit_bytes=64 * 1000 * 1000),
         cost_estimate=pl.CostEstimate(flops=flops, bytes_accessed=4 * 3 * n_exp * width * ff * 2, transcendentals=0),
@@ -432,9 +438,10 @@
         chunks = []
         layer_outs = []
         for layer_idx in range(n_stage):
-            meta = round_meta(layer_idx, n_stage, n_group)
-            meta, all_mix, normed = lax.optimization_barrier((meta, all_mix, normed))
-            chunks += send_round(layer_idx, meta, *weights, n_stage, n_group)
+            if layer_idx == 0:
+                for r in range(n_stage):
+                    meta, all_mix, normed = lax.optimization_barrier((round_meta(r, n_stage, n_group), all_mix, normed))
+                    chunks += send_round(r, meta, *weights, n_stage, n_group)
             layer_mix = all_mix[:, layer_idx]
             layer_mix = layer_mix[::-1] if layer_idx else layer_mix
             mine = lax.dynamic_slice_in_dim(layer_mix.reshape(-1, n_experts), group_idx * exp_loc, exp_loc, axis=1)

time: 1490 us -> 1340 us (0.90)
  the two profiles are of different devices: /device:TPU:2 before, /device:TPU:0 now
where the time goes in v2:
time: 1340 us
  Pallas kernels  1180 us (88%)
  starting transfers between devices  125 us (9%)
  other arithmetic  16.3 us (1%)
  blocking collectives  14.4 us (1%)
    pallas_call x2, Pallas kernels, moe_layer(): pl.pallas_call(functools.partial(moe_body, layer_idx, (n_group, rows, wid...  1010 us
    ppermute x12, starting transfers between devices, send_round(): landed = lax.ppermute(own, FLAT, pairs)  125 us
    pallas_call x12, Pallas kernels, pick(): pl.pallas_call(functools.partial(body, row_start, n), out_shape=jax.Shape...  83.2 us
    pallas_call x12, Pallas kernels, place(): pl.pallas_call(functools.partial(place_body, row_start, n), out_shape=jax...  82.9 us
  transfers between devices with their start and end apart: 12, of which 0 were waited for; matrix products, arithmetic and copies ran while one was open for 1% of the time, Pallas kernels for 87%

profile of v2, /device:TPU:0, one launch (start us, length us, event | category | flops | bytes accessed | tf_op | source)
XLA Modules:
  0.0 1339.7 jit_solution(16157556532836111912)
XLA Ops:
  6.4 14.4 %all-gather = f32[16,256,16]{1,2,0:T(8,128)S(1)} all-gather(f32[2,256,16]{1,2,0:T(8,128)S(1)} %select_reduce_fusion), channel_id=2, replica_groups=mesh['stage'=2,'expert'=4] {'stage','expert'}, dimensions={0}, use_global_device_ids=true | all-gather | bytes 294912 | tf_op jit(solution)/shard_map/all_gather | solution.py:435
  21.5 6.9 shard_map.92.own_ref
  32.1 6.9 shard_map.91.own_ref
  42.7 6.9 shard_map.90.own_ref
  49.6 3.8 collective-permute-start.5
  53.4 6.9 shard_map.89.own_ref
  60.3 3.8 collective-permute-start.4
  64.8 6.8 shard_map.88.own_ref
  75.0 6.9 shard_map.87.own_ref
  81.9 7.0 shard_map.104.own_ref
  88.9 27.8 %collective-permute-start.2 = (bf16[2,640,3072]{2,1,0:T(8,128)(2,1)}, bf16[2,640,3072]{2,1,0:T(8,128)(2,1)}, u32[]{:S(2)}, u32[]{:S(2)}) collective-permute-start(bf16[2,640,3072]{2,1,0:T(8,128)(2,1)} %shard_map.87.own_ref), channel_id=1, source_target_pairs={{0,1},{1,3},{2,5},{3,7},{4,0},{5,2},{6,4},{7,6}} | collective-permute-start | bytes 23592968 | tf_op jit(solution)/shard_map/ppermute | solution.py:137
  120.5 550.1 %shard_map.109 = (f32[2,256,2560]{2,1,0:T(8,128)}, f32[3,512,2560]{2,1,0:T(8,128)}) custom-call(bf16[256,2560]{1,0:T(8,128)(2,1)} %fusion.1.u_ref, f32[2048,128]{1,0:T(8,128)} %pad.7.mix_ref, bf16[4,2560,1536]{2,1,0:T(8,128)(2,1)} %bitcast.30, bf16[4,2560,1536]{2,1,0:T(8,128)(2,1)} %bitcast.40, bf16[4,1536,2560]{2,1,0:T(8,128)(2,1)} %bitcast.45), custom_call_target="tpu_custom_call" | custom-call | flops 193273528320 | bytes 377487360 | tf_op jit(solution)/shard_map/pallas_call | solution.py:400
  675.1 7.1 shard_map.86.own_ref
  682.2 6.9 shard_map.85.own_ref
  689.1 7.0 shard_map.103.own_ref
  696.1 7.0 shard_map.102.own_ref
  703.1 7.0 shard_map.101.own_ref
  711.4 3.8 collective-permute-start.10
  716.5 73.6 %collective-permute-start.8 = (bf16[2,768,2560]{2,1,0:T(8,128)(2,1)}, bf16[2,768,2560]{2,1,0:T(8,128)(2,1)}, u32[]{:S(2)}, u32[]{:S(2)}) collective-permute-start(bf16[2,768,2560]{2,1,0:T(8,128)(2,1)} %shard_map.101.own_ref), channel_id=1, source_target_pairs={{0,1},{1,3},{2,5},{3,7},{4,0},{5,2},{6,4},{7,6}} | collective-permute-start | bytes 23592968 | tf_op jit(solution)/shard_map/ppermute | solution.py:137
  790.1 460.5 %shard_map.110 = (f32[2,256,2560]{2,1,0:T(8,128)}, f32[3,512,2560]{2,1,0:T(8,128)}) custom-call(bf16[256,2560]{1,0:T(8,128)(2,1)} %multiply_convert_fusion.u_ref, f32[2048,128]{1,0:T(8,128)} %pad.8.mix_ref, bf16[4,2560,1536]{2,1,0:T(8,128)(2,1)} %bitcast.33, bf16[4,2560,1536]{2,1,0:T(8,128)(2,1)} %bitcast.43, bf16[4,1536,2560]{2,1,0:T(8,128)(2,1)} %bitcast.49), custom_call_target="tpu_custom_call" | custom-call | flops 193273528320 | bytes 377487360 | tf_op jit(solution)/shard_map/pallas_call | solution.py:400
  1256.6 6.9 shard_map.93.rest_0_
  1263.6 6.9 shard_map.105.rest_0_
  1270.5 6.9 shard_map.94.rest_0_
  1277.4 6.9 shard_map.95.rest_0_
  1284.4 6.9 shard_map.96.rest_0_
  1291.3 6.9 shard_map.97.rest_0_
  1298.2 6.9 shard_map.98.rest_0_
  1305.1 6.9 shard_map.99.rest_0_
  1312.0 6.9 shard_map.100
  1318.9 6.9 shard_map.106.rest_0_
  1325.9 6.9 shard_map.107.rest_0_
  1332.8 6.9 shard_map.108
  (45 shorter events, 34.6 us)
Async XLA Ops:
  28.4 60.6 %collective-permute-start.7 = (bf16[2,640,3072]{2,1,0:T(8,128)(2,1)}, bf16[2,640,3072]{2,1,0:T(8,128)(2,1)}, u32[]{:S(2)}, u32[]{:S(2)}) collective-permute-start(bf16[2,640,3072]{2,1,0:T(8,128)(2,1)} %shard_map.92.own_ref), channel_id=1, source_target_pairs={{1,2},{2,4},{3,6},{4,1},{5,3},{6,5}} | collective-permute-start | bytes 23592968 | tf_op jit(solution)/shard_map/ppermute | solution.py:137
  39.0 77.7 %collective-permute-start.6 = (bf16[2,640,3072]{2,1,0:T(8,128)(2,1)}, bf16[2,640,3072]{2,1,0:T(8,128)(2,1)}, u32[]{:S(2)}, u32[]{:S(2)}) collective-permute-start(bf16[2,640,3072]{2,1,0:T(8,128)(2,1)} %shard_map.91.own_ref), channel_id=1, source_target_pairs={{1,2},{2,4},{3,6},{4,1},{5,3},{6,5}} | collective-permute-start | bytes 23592968 | tf_op jit(solution)/shard_map/ppermute | solution.py:137
  49.6 661.8 %collective-permute-start.5 = (bf16[2,640,3072]{2,1,0:T(8,128)(2,1)}, bf16[2,640,3072]{2,1,0:T(8,128)(2,1)}, u32[]{:S(2)}, u32[]{:S(2)}) collective-permute-start(bf16[2,640,3072]{2,1,0:T(8,128)(2,1)} %shard_map.90.own_ref), channel_id=1, source_target_pairs={{1,2},{2,4},{3,6},{4,1},{5,3},{6,5}} | collective-permute-start | bytes 23592968 | tf_op jit(solution)/shard_map/ppermute | solution.py:137
  60.3 651.0 %collective-permute-start.4 = (bf16[2,640,3072]{2,1,0:T(8,128)(2,1)}, bf16[2,640,3072]{2,1,0:T(8,128)(2,1)}, u32[]{:S(2)}, u32[]{:S(2)}) collective-permute-start(bf16[2,640,3072]{2,1,0:T(8,128)(2,1)} %shard_map.89.own_ref), channel_id=1, source_target_pairs={{1,2},{2,4},{3,6},{4,1},{5,3},{6,5}} | collective-permute-start | bytes 23592968 | tf_op jit(solution)/shard_map/ppermute | solution.py:137
  71.6 639.8 %collective-permute-start.3 = (bf16[2,640,3072]{2,1,0:T(8,128)(2,1)}, bf16[2,640,3072]{2,1,0:T(8,128)(2,1)}, u32[]{:S(2)}, u32[]{:S(2)}) collective-permute-start(bf16[2,640,3072]{2,1,0:T(8,128)(2,1)} %shard_map.88.own_ref), channel_id=1, source_target_pairs={{0,1},{1,3},{2,5},{3,7},{4,0},{5,2},{6,4},{7,6}} | collective-permute-start | bytes 23592968 | tf_op jit(solution)/shard_map/ppermute | solution.py:137
  88.9 626.3 %collective-permute-start.2 = (bf16[2,640,3072]{2,1,0:T(8,128)(2,1)}, bf16[2,640,3072]{2,1,0:T(8,128)(2,1)}, u32[]{:S(2)}, u32[]{:S(2)}) collective-permute-start(bf16[2,640,3072]{2,1,0:T(8,128)(2,1)} %shard_map.87.own_ref), channel_id=1, source_target_pairs={{0,1},{1,3},{2,5},{3,7},{4,0},{5,2},{6,4},{7,6}} | collective-permute-start | bytes 23592968 | tf_op jit(solution)/shard_map/ppermute | solution.py:137
  116.7 599.8 %collective-permute-start.11 = (bf16[2,768,2560]{2,1,0:T(8,128)(2,1)}, bf16[2,768,2560]{2,1,0:T(8,128)(2,1)}, u32[]{:S(2)}, u32[]{:S(2)}) collective-permute-start(bf16[2,768,2560]{2,1,0:T(8,128)(2,1)} %shard_map.104.own_ref), channel_id=1, source_target_pairs={{1,2},{2,4},{3,6},{4,1},{5,3},{6,5}} | collective-permute-start | bytes 23592968 | tf_op jit(solution)/shard_map/ppermute | solution.py:137
  120.5 550.2 %copy-start.2 = (f32[2048,4]{1,0:T(8,128)S(1)}, f32[2048,4]{1,0:T(8,128)}, u32[]{:S(2)}) copy-start(f32[2048,4]{1,0:T(8,128)} %get-tuple-element.23) | copy-start | bytes 98308
  675.1 35.0 %copy-start = (f32[256,2560]{1,0:T(8,128)}, f32[256,2560]{1,0:T(8,128)S(1)}, u32[]{:S(2)}) copy-start(f32[256,2560]{1,0:T(8,128)S(1)} %get-tuple-element.20) | copy-start | bytes 7864324
  711.3 593.8 %collective-permute-start.1 = (bf16[2,640,3072]{2,1,0:T(8,128)(2,1)}, bf16[2,640,3072]{2,1,0:T(8,128)(2,1)}, u32[]{:S(2)}, u32[]{:S(2)}) collective-permute-start(bf16[2,640,3072]{2,1,0:T(8,128)(2,1)} %shard_map.86.own_ref), channel_id=1, source_target_pairs={{0,1},{1,3},{2,5},{3,7},{4,0},{5,2},{6,4},{7,6}} | collective-permute-start | bytes 23592968 | tf_op jit(solution)/shard_map/ppermute | solution.py:137
  711.4 600.7 %collective-permute-start = (bf16[2,640,3072]{2,1,0:T(8,128)(2,1)}, bf16[2,640,3072]{2,1,0:T(8,128)(2,1)}, u32[]{:S(2)}, u32[]{:S(2)}) collective-permute-start(bf16[2,640,3072]{2,1,0:T(8,128)(2,1)} %shard_map.85.own_ref), channel_id=1, source_target_pairs={{0,1},{1,3},{2,5},{3,7},{4,0},{5,2},{6,4},{7,6}} | collective-permute-start | bytes 23592968 | tf_op jit(solution)/shard_map/ppermute | solution.py:137
  711.4 607.5 %collective-permute-start.10 = (bf16[2,768,2560]{2,1,0:T(8,128)(2,1)}, bf16[2,768,2560]{2,1,0:T(8,128)(2,1)}, u32[]{:S(2)}, u32[]{:S(2)}) collective-permute-start(bf16[2,768,2560]{2,1,0:T(8,128)(2,1)} %shard_map.103.own_ref), channel_id=1, source_target_pairs={{1,2},{2,4},{3,6},{4,1},{5,3},{6,5}} | collective-permute-start | bytes 23592968 | tf_op jit(solution)/shard_map/ppermute | solution.py:137
  715.2 610.6 %collective-permute-start.9 = (bf16[2,768,2560]{2,1,0:T(8,128)(2,1)}, bf16[2,768,2560]{2,1,0:T(8,128)(2,1)}, u32[]{:S(2)}, u32[]{:S(2)}) collective-permute-start(bf16[2,768,2560]{2,1,0:T(8,128)(2,1)} %shard_map.102.own_ref), channel_id=1, source_target_pairs={{0,1},{1,3},{2,5},{3,7},{4,0},{5,2},{6,4},{7,6}} | collective-permute-start | bytes 23592968 | tf_op jit(solution)/shard_map/ppermute | solution.py:137
  716.5 616.3 %collective-permute-start.8 = (bf16[2,768,2560]{2,1,0:T(8,128)(2,1)}, bf16[2,768,2560]{2,1,0:T(8,128)(2,1)}, u32[]{:S(2)}, u32[]{:S(2)}) collective-permute-start(bf16[2,768,2560]{2,1,0:T(8,128)(2,1)} %shard_map.101.own_ref), channel_id=1, source_target_pairs={{0,1},{1,3},{2,5},{3,7},{4,0},{5,2},{6,4},{7,6}} | collective-permute-start | bytes 23592968 | tf_op jit(solution)/shard_map/ppermute | solution.py:137
  790.1 460.5 %copy-start.1 = (f32[256,2560]{1,0:T(8,128)S(1)}, f32[256,2560]{1,0:T(8,128)}, u32[]{:S(2)}) copy-start(f32[256,2560]{1,0:T(8,128)} %copy-done) | copy-start | bytes 7864324
